TPU v7x, 128 devices: a whole 4x4x4 slice. The times are simulated.
128 devices in a mesh: cp: 64 (over x, z, y), hd: 2 (over core).
Axes of the slice: x: 4, y: 4, z: 4, core: 2. Of those that a mesh axis runs over, the one named last changes fastest.
Arguments:
- queries: bfloat16 [12288, 4096], P('cp', 'hd'), may hold values from -48 to 48
- keys: bfloat16 [12288, 1024], P('cp', 'hd'), may hold values from -48 to 48
- values: bfloat16 [12288, 1024], P('cp', 'hd'), may hold values from -6 to 6
- span_table: int32 [128], replicated, may hold values from 0 to 127, as said below
- doc_ids: int32 [12288], replicated, may hold values from 0 to 7, never falling along the last dimension, each value on 1 to 3072 neighbouring positions
- out_weight: bfloat16 [4096, 4096], P('hd'), may hold values from -0.09375 to 0.09375
Outputs:
- mixed: bfloat16 [12288, 4096], P(('cp', 'hd'))
Inputs may be any that keep to these rules, and one draw needn't show every extreme that they name: `span_table`: slots 2 j and 2 j + 1 hold two spans c and 127 - c, and every span is held once.
All inputs are finite; a program needn't handle non-finite values.
Results may differ from a plain program's by a relative error of at most 0.0095.
Values may be sent and summed in bfloat16 or wider, within the bound.
A program may use at most 128 MiB of HBM per device.

v0:
```python
import functools
import math

import jax
import jax.numpy as jnp
from jax import lax
from jax.experimental import pallas as pl
from jax.experimental.pallas import tpu as pltpu
from jax.sharding import PartitionSpec as P

HEAD_WIDTH = 128
DOCS = 8
LANES = 256
NEG = -1e30
MESH = pl.DeviceIdType.MESH


def kernel(
    line, q_ref, span_ref, doc_ref, k_hbm, v_hbm, w_hbm, out_ref,
    kv, w_vmem, q_t, acc, best, total, fades, held, bias, low, high, attn, outgoing, incoming, kept,
    load_sem, w_sem, send0, send_z, send_xy, recv, out_send, out_recv,
):
    rows = q_ref.shape[0]
    span_len = rows // 2
    kv_heads = k_hbm.shape[1] // HEAD_WIDTH
    group = q_ref.shape[1] // HEAD_WIDTH // kv_heads
    tiles = group * rows // LANES
    whole = rows // 3
    side = (rows - whole) // 2
    me = lax.axis_index("cp")
    hd = lax.axis_index("hd")
    z = me // 4
    y = (me // 2) % 2
    x = me % 2

    def slot(zz, fx, fy):
        xx = 1 - x if fx else x
        yy = 1 - y if fy else y
        return zz * 4 + yy * 2 + xx

    piece_rows = {
        "A": (0, side, 0), "B": (side, side, 1), "C": (2 * side, whole, 2),
        "C0": (2 * side, whole // 2, 2), "C1": (2 * side + whole // 2, whole // 2, 3),
    }

    def part(src, piece):
        start, size, _ = piece_rows[piece]
        return kv.at[src, :, pl.ds(start, size), :]

    def copy_of(src, piece, target, sem):
        return pltpu.make_async_remote_copy(
            src_ref=part(src, piece), dst_ref=part(src, piece), send_sem=sem,
            recv_sem=recv.at[src, piece_rows[piece][2]],
            device_id={"cp": target}, device_id_type=MESH,
        )

    def arrived(src, piece):
        copy_of(src, piece, slot(z, True, False), send0.at[0]).wait_recv()

    to_x, to_y = slot(z, True, False), slot(z, False, True)
    up, down = me + 4, me - 4
    has_up, has_down = z < line - 1, z > 0

    loads = [
        pltpu.make_async_copy(k_hbm, kv.at[me, 0], load_sem.at[0]),
        pltpu.make_async_copy(v_hbm, kv.at[me, 1], load_sem.at[1]),
    ]
    w_load = pltpu.make_async_copy(w_hbm, w_vmem, w_sem)
    for load in loads:
        load.start()
    barrier = pltpu.get_barrier_semaphore()
    for target in (to_x, to_y):
        pl.semaphore_signal(barrier, inc=1, device_id={"cp": target}, device_id_type=MESH)
    pl.semaphore_signal(barrier, inc=1, device_id={"hd": 1 - hd}, device_id_type=MESH)

    @pl.when(has_up)
    def _():
        pl.semaphore_signal(barrier, inc=1, device_id={"cp": up}, device_id_type=MESH)

    @pl.when(has_down)
    def _():
        pl.semaphore_signal(barrier, inc=1, device_id={"cp": down}, device_id_type=MESH)

    pl.semaphore_wait(barrier, 3 + has_up.astype(jnp.int32) + has_down.astype(jnp.int32))
    for load in loads:
        load.wait()

    own, xn, yn, dg = (False, False), (True, False), (False, True), (True, True)
    first_x = [(own, "A"), (own, "C"), (own, "B")]
    first_y = [(own, "B"), (own, "C"), (own, "A")]
    first_z = [(own, "C"), (own, "A"), (own, "B")]
    later_z = [(xn, "A"), (yn, "B")]

    def first_stage(act, xs, ys, zs, nx, ny, nz):
        for i in range(max(len(xs), len(ys))):
            if i < len(xs):
                act(copy_of(slot(z, *xs[i][0]), xs[i][1], to_x, send0.at[nx + i]))
            if i < len(ys):
                act(copy_of(slot(z, *ys[i][0]), ys[i][1], to_y, send0.at[5 + ny + i]))

        @pl.when(has_up)
        def _():
            for i, (flips, piece) in enumerate(zs):
                act(copy_of(slot(z, *flips), piece, up, send0.at[10 + nz + i]))

        @pl.when(has_down)
        def _():
            for i, (flips, piece) in enumerate(zs):
                act(copy_of(slot(z, *flips), piece, down, send0.at[15 + nz + i]))

    def go(copy):
        copy.start()

    def sent(copy):
        copy.wait_send()

    first_stage(go, first_x, first_y, first_z, 0, 0, 0)
    w_load.start()

    lane = lax.broadcasted_iota(jnp.int32, (1, tiles * LANES), 1) % rows
    span0, span1 = span_ref[2 * me], span_ref[2 * me + 1]
    row_pos = jnp.where(lane < span_len, span0 * span_len + lane, (span1 - 1) * span_len + lane)
    row_pos = row_pos.astype(jnp.float32)
    row_low = jnp.zeros_like(row_pos)
    docs = doc_ref[...]
    for d in range(1, DOCS):
        start = jnp.sum(jnp.where(docs < d, 1.0, 0.0), keepdims=True)
        row_low = jnp.maximum(row_low, jnp.where(start <= row_pos, start, 0.0))
    for c in range(tiles):
        low[c] = row_low[:, c * LANES:(c + 1) * LANES]
        high[c] = row_pos[:, c * LANES:(c + 1) * LANES]
    for g in range(kv_heads):
        heads = [q_ref[:, (g * group + h) * HEAD_WIDTH:(g * group + h + 1) * HEAD_WIDTH] for h in range(group)]
        flipped = jnp.concatenate(heads, axis=0).T
        for c in range(tiles):
            q_t[g, c] = flipped[:, c * LANES:(c + 1) * LANES]

    factor = HEAD_WIDTH ** (-0.5) * math.log2(math.e)

    def attend(src, initial=False):
        s0, s1 = span_ref[2 * src], span_ref[2 * src + 1]
        key = lax.broadcasted_iota(jnp.int32, (rows, LANES), 0)
        key_pos = jnp.where(key < span_len, s0 * span_len, (s1 - 1) * span_len) + key
        key_pos = key_pos.astype(jnp.float32)
        for c in range(tiles):
            visible = (key_pos >= low[c]) & (key_pos <= high[c])
            bias[c] = jnp.where(visible, 0.0, NEG)

        def weigh(g):
            keys = kv[src, 0, :, g * HEAD_WIDTH:(g + 1) * HEAD_WIDTH]
            for c in range(tiles):
                scores = jnp.dot(keys, q_t[g, c], preferred_element_type=jnp.float32)
                scores = scores * factor + bias[c]
                top = jnp.max(scores, axis=0, keepdims=True)
                if not initial:
                    old = best[g, c]
                    top = jnp.maximum(old, top)
                    fade = jnp.exp2(old - top)
                    fades[g, c] = fade
                weights = jnp.exp2(scores - top)
                weight_sum = jnp.sum(weights, axis=0, keepdims=True)
                best[g, c] = top
                total[g, c] = weight_sum if initial else total[g, c] * fade + weight_sum
                held[g, c] = weights.astype(jnp.bfloat16)

        def gather(g):
            values = kv[src, 1, :, g * HEAD_WIDTH:(g + 1) * HEAD_WIDTH].T
            for c in range(tiles):
                part_sum = jnp.dot(values, held[g, c], preferred_element_type=jnp.float32)
                acc[g, c] = part_sum if initial else acc[g, c] * fades[g, c] + part_sum

        for g in range(kv_heads):
            weigh(g)
            if g:
                gather(g - 1)
        gather(kv_heads - 1)

    attend(me, initial=True)

    arrived(slot(z, *xn), "A")
    arrived(slot(z, *yn), "B")
    first_stage(go, [(yn, "B")], [(xn, "A")], later_z, 3, 3, 3)
    arrived(slot(z, *xn), "C")
    arrived(slot(z, *yn), "C")
    first_stage(go, [(yn, "C0")], [(xn, "C1")], [], 4, 4, 0)
    near = jnp.minimum(z, line - 1 - z)

    def plane(j):
        both = jnp.where(j % 2 == 1, z + (j + 1) // 2, z - j // 2)
        rest = jnp.where(z < line - 1 - z, j, line - 1 - j)
        return jnp.where(j <= 2 * near, both, rest)

    def sides(i, fn):
        @pl.when(z - i >= 0)
        def _():
            fn(z - i, 0, has_up, up)

        @pl.when((z + i < line) & (i > 0))
        def _():
            fn(z + i, 1, has_down, down)

    z_pieces = [(own, "C", "xy"), (own, "A", "y"), (own, "B", "x"), (xn, "A", "y"), (yn, "B", "x")]

    def z_step(i, n, act):
        flips, piece, links = z_pieces[n]

        def fn(zz, side, can, target):
            src = slot(zz, *flips)
            if act is go:
                arrived(src, piece)

            @pl.when(can)
            def _():
                act(copy_of(src, piece, target, send_z.at[i - 1, side, n]))

            if "x" in links:
                act(copy_of(src, piece, to_x, send_xy.at[i - 1, side, 0, min(n, 2)
                                                         if n != 4 else 1]))
            if "y" in links:
                act(copy_of(src, piece, to_y, send_xy.at[i - 1, side, 1, min(n, 2)]))

        sides(i, fn)

    def corner_step(i, act):
        def fn(zz, side, can, target):
            src_x, src_y = slot(zz, *xn), slot(zz, *yn)
            if act is go:
                arrived(src_x, "C")
            act(copy_of(src_x, "C1", to_y, send_xy.at[i - 1, side, 1, 3]))
            if act is go:
                arrived(src_y, "C")
            act(copy_of(src_y, "C0", to_x, send_xy.at[i - 1, side, 0, 3]))

        sides(i, fn)

    def wait_step(i, flips, pieces):
        def fn(zz, side, can, target):
            for piece in pieces:
                arrived(slot(zz, *flips), piece)

        sides(i, fn)

    dg_pieces = ("B", "A", "C0", "C1")

    def finish(i):
        here = plane(i)
        for flips, pieces in ((xn, ("B",)), (yn, ("A",)), (dg, dg_pieces)):
            wait_step(i, flips, pieces)
            attend(slot(here, *flips))

    def stage(i, carry, last=False):
        z_step(i, 0, go)
        z_step(i, 1, go)

        @pl.when(i > 1)
        def _():
            corner_step(i - 1, go)

        z_step(i, 2, go)
        if last:
            finish(i - 1)
            attend(slot(plane(i), *own))
        z_step(i, 3, go)
        z_step(i, 4, go)
        if not last:
            attend(slot(plane(i), *own))
            finish(i - 1)
        return carry

    lax.fori_loop(1, line - 1, stage, 0)
    stage(line - 1, 0, last=True)
    corner_step(line - 1, go)
    finish(line - 1)

    for g in range(kv_heads):
        parts = [acc[g, c] / total[g, c] for c in range(tiles)]
        turned = jnp.concatenate(parts, axis=1).T.astype(jnp.bfloat16)
        for h in range(group):
            first = (g * group + h) * HEAD_WIDTH
            attn[:, first:first + HEAD_WIDTH] = turned[h * rows:(h + 1) * rows]

    w_load.wait()
    half = rows // 2
    count, width = outgoing.shape[0], outgoing.shape[2]

    def hand_over(n):
        return pltpu.make_async_remote_copy(
            src_ref=outgoing.at[n], dst_ref=incoming.at[n], send_sem=out_send.at[n],
            recv_sem=out_recv.at[n], device_id={"hd": 1 - hd}, device_id_type=MESH,
        )

    @pl.loop(0, count)
    def _(n):
        columns = pl.ds(pl.multiple_of(n * width, width), width)
        product = jnp.dot(attn[...], w_vmem[:, columns], preferred_element_type=jnp.float32)
        upper, lower = product[:half], product[half:]
        mine = hd == 0
        outgoing[n] = jnp.where(mine, lower, upper).astype(jnp.bfloat16)
        kept[n] = jnp.where(mine, upper, lower)
        hand_over(n).start()

    for n in range(count):
        hand_over(n).wait_recv()
        out_ref[:, n * width:(n + 1) * width] = (kept[n] + incoming[n].astype(jnp.float32)).astype(jnp.bfloat16)

    for n in range(count):
        hand_over(n).wait_send()
    first_stage(sent, first_x, first_y, first_z, 0, 0, 0)
    first_stage(sent, [(yn, "B")], [(xn, "A")], later_z, 3, 3, 3)
    first_stage(sent, [(yn, "C0")], [(xn, "C1")], [], 4, 4, 0)

    def drain(i, carry):
        for n in range(5):
            z_step(i, n, sent)
        corner_step(i, sent)
        return carry

    lax.fori_loop(1, line, drain, 0)


def local(cp, queries, keys, values, span_table, doc_ids, out_weight):
    rows = queries.shape[0]
    kv_heads = keys.shape[1] // HEAD_WIDTH
    group = queries.shape[1] // HEAD_WIDTH // kv_heads
    tiles = group * rows // LANES
    line = cp // 4
    model = out_weight.shape[1]
    count = 8
    width = model // count
    half = rows // 2
    vmem, hbm = pltpu.VMEM, pl.ANY
    spec = lambda space: pl.BlockSpec(memory_space=space)
    dma = pltpu.SemaphoreType.DMA
    f32, bf16 = jnp.float32, jnp.bfloat16
    return pl.pallas_call(
        functools.partial(kernel, line),
        out_shape=jax.ShapeDtypeStruct((half, model), bf16),
        in_specs=[spec(vmem), spec(pltpu.SMEM), spec(vmem), spec(hbm), spec(hbm), spec(hbm)],
        out_specs=spec(vmem),
        scratch_shapes=[
            vmem((cp, 2, rows, keys.shape[1]), bf16),
            vmem(out_weight.shape, bf16),
            vmem((kv_heads, tiles, HEAD_WIDTH, LANES), bf16),
            vmem((kv_heads, tiles, HEAD_WIDTH, LANES), f32),
            vmem((kv_heads, tiles, 1, LANES), f32),
            vmem((kv_heads, tiles, 1, LANES), f32),
            vmem((kv_heads, tiles, 1, LANES), f32),
            vmem((kv_heads, tiles, rows, LANES), bf16),
            vmem((tiles, rows, LANES), f32),
            vmem((tiles, 1, LANES), f32),
            vmem((tiles, 1, LANES), f32),
            vmem((rows, queries.shape[1]), bf16),
            vmem((count, half, width), bf16),
            vmem((count, half, width), bf16),
            vmem((count, half, width), f32),
            dma((2,)), dma, dma((20,)), dma((line, 2, 5)), dma((line, 2, 2, 4)),
            dma((cp, 4)), dma((count,)), dma((count,)),
        ],
        compiler_params=pltpu.CompilerParams(
            collective_id=0, has_side_effects=True, vmem_limit_bytes=60 * 2 ** 20,
        ),
    )(queries, span_table, doc_ids.reshape(-1, 128), keys, values, out_weight)


def solution(mesh):
    return jax.shard_map(
        functools.partial(local, mesh.shape["cp"]),
        mesh=mesh,
        in_specs=(P("cp", "hd"), P("cp", "hd"), P("cp", "hd"), P(), P(), P("hd", None)),
        out_specs=P(("cp", "hd"), None),
        check_vma=False,
    )
```

profile of v0, /device:TPU:5, one launch (start us, length us, event | category | flops | bytes accessed | tf_op | source)
XLA Modules:
  0.0 378.1 jit_solution(16849678909068322937)
XLA Ops:
  0.0 376.1 %shard_map.64 = bf16[96,4096]{1,0:T(8,128)(2,1)} custom-call(bf16[192,2048]{1,0:T(8,128)(2,1)} %q_ref.1, s32[128]{0:T(128)} %span_ref.1, s32[96,128]{1,0:T(8,128)} %bitcast.1, bf16[192,512]{1,0:T(8,128)(2,1)} %k_hbm.1, bf16[192,512]{1,0:T(8,128)(2,1)} %v_hbm.1, bf16[2048,4096]{1,0:T(8,128)(2,1)} %w_hbm.1), custom_call_target="tpu_custom_call" | custom-call | tf_op jit(solution)/shard_map/pallas_call | solution.py:335
  376.1 2.1 copy.8
where the time goes:
time: 378 us
  Pallas kernels  376 us (99%)
    pallas_call x1, Pallas kernels, local(): pl.pallas_call(functools.partial(kernel, line), out_shape=jax.ShapeDtypeS...  376 us

commit v1 on v0

v1 whole, which is shorter than its diff:
```python
import functools
import math

import jax
import jax.numpy as jnp
from jax import lax
from jax.experimental import pallas as pl
from jax.experimental.pallas import tpu as pltpu
from jax.sharding import PartitionSpec as P

WIDTH = 128
SPAN = 96
GROUP = 4
ROWS = GROUP * SPAN
PIECES = 8
DOCS = 8
BACK = 32
STEP = 8
KEYS = STEP * SPAN
STEPS = BACK // STEP
NEG = -1e30
MESH = pl.DeviceIdType.MESH
FACTOR = WIDTH ** -0.5 * math.log2(math.e)
ARRIVAL = (0, 1, 3, 4, 2, 5, 7, 6)
EARLY = (0, 1, 3, 4, 2)
RETURN = (6, 5, 7, 2, 4, 1, 3, 0)


def kernel(
    span_ref, span_row_ref, doc_ref, q_hbm, k_hbm, v_hbm, w_hbm, out_ref,
    q_in, k_in, v_in, kv, q_buf, o_buf, attn, w_vmem, scores, own_acc, own_top, penalty, table,
    outgoing, incoming, kept, index,
    load_sem, local_sem, w_sem, table_sem,
    su, sq, ru, rq, s_own, s_far, s_half, s_z, rx, rz, sd, rd, so, ro, xs, xr,
):
    me = lax.axis_index("cp")
    hd = lax.axis_index("hd")
    other = 1 - hd
    x, z, y = me // 16, (me // 4) % 4, me % 4
    home = (z // 2) == hd
    zp = z + 1 - 2 * (z % 2)

    def chip(xx, zz, yy):
        return xx * 16 + zz * 4 + yy

    right, left, across = chip((x + 1) % 4, z, y), chip((x + 3) % 4, z, y), chip(x, zp, y)

    def source(xo, zo, i):
        return chip(xo, 3 - zo if i >= 4 else zo, (y + i % 4) % 4)

    def remote(src, dst, send, recv, cp, core):
        return pltpu.make_async_remote_copy(
            src_ref=src, dst_ref=dst, send_sem=send, recv_sem=recv,
            device_id={"cp": cp, "hd": core}, device_id_type=MESH,
        )

    def landed(dst, sem):
        remote(dst, dst, sd.at[0], sem, me, other).wait_recv()

    def go(copy):
        copy.start()

    def sent(copy):
        copy.wait_send()

    my_rows = pl.ds(pl.multiple_of(hd * SPAN, SPAN), SPAN)
    my_head = pl.ds(pl.multiple_of(y * WIDTH, WIDTH), WIDTH)
    my_queries = pl.ds(pl.multiple_of(y * GROUP * WIDTH, GROUP * WIDTH), GROUP * WIDTH)

    loads = [
        pltpu.make_async_copy(k_hbm, k_in, load_sem.at[0]),
        pltpu.make_async_copy(v_hbm, v_in, load_sem.at[1]),
        pltpu.make_async_copy(q_hbm, q_in, load_sem.at[2]),
    ]
    locals_ = [
        pltpu.make_async_copy(k_hbm.at[my_rows, my_head], kv.at[2 * me + hd, 0], ru.at[0, 0]),
        pltpu.make_async_copy(v_hbm.at[my_rows, my_head], kv.at[2 * me + hd, 1], ru.at[0, 1]),
        pltpu.make_async_copy(q_hbm.at[my_rows, my_queries], q_buf.at[0], rq.at[0]),
    ]
    w_load = pltpu.make_async_copy(w_hbm, w_vmem, w_sem)
    for load in loads:
        load.start()

    barrier = pltpu.get_barrier_semaphore()

    def greet(cp, core):
        pl.semaphore_signal(barrier, inc=1, device_id={"cp": cp, "hd": core}, device_id_type=MESH)

    for i in range(PIECES):
        for core in (hd, other):
            if i or core is other:
                greet(source(x, z, i), core)
    for target in (right, left, across):
        greet(target, hd)

    spans = jnp.broadcast_to(span_row_ref[...].astype(jnp.float32), (128, 128)).T
    held_by = lax.broadcasted_iota(jnp.int32, (128, 128), 0).astype(jnp.float32)
    wanted = lax.broadcasted_iota(jnp.int32, (128, 128), 1).astype(jnp.float32)
    table[0:1, :] = jnp.max(jnp.where(spans == wanted, held_by, 0.0), axis=0, keepdims=True).astype(jnp.int32)
    docs = doc_ref[...]
    lane = lax.broadcasted_iota(jnp.int32, (1, 128), 1)
    starts = jnp.zeros((1, 128), jnp.float32)
    for d in range(1, DOCS):
        first = jnp.sum(jnp.where(docs < d, 1.0, 0.0), keepdims=True)
        starts = jnp.where(lane == d, first, starts)
    table[1:2, :] = starts.astype(jnp.int32)

    pl.semaphore_wait(barrier, 2 * PIECES + 2)

    tz = jnp.where(home, z, 3 - z)

    def scatter(act, what):
        for dj in (0, 1, 3, 2):
            j = (y + dj) % 4
            to = chip(x, tz, j)
            piece = jnp.where(home, 0, 4) + (4 - dj) % 4
            for rel, core in enumerate((hd, other)):
                rows = pl.ds(pl.multiple_of(core * SPAN, SPAN), SPAN)

                def one():
                    if what == "kv":
                        columns = pl.ds(pl.multiple_of(j * WIDTH, WIDTH), WIDTH)
                        for v, staged in enumerate((k_in, v_in)):
                            act(remote(staged.at[rows, columns], kv.at[2 * me + core, v],
                                       su.at[dj, rel, v], ru.at[piece, v], to, core))
                    else:
                        columns = pl.ds(pl.multiple_of(j * GROUP * WIDTH, GROUP * WIDTH), GROUP * WIDTH)
                        act(remote(q_in.at[rows, columns], q_buf.at[piece],
                                   sq.at[dj, rel], rq.at[piece], to, core))

                if dj == 0 and rel == 0:
                    pl.when(jnp.logical_not(home))(one)
                else:
                    one()

    @pl.when(home)
    def _():
        for copy in locals_:
            copy.start()

    loads[0].wait()
    loads[1].wait()
    scatter(go, "kv")
    loads[2].wait()
    scatter(go, "q")
    w_load.start()
    table_copy = pltpu.make_async_copy(table, index, table_sem)

    def piece_of(xo, zo, i):
        return kv.at[2 * source(xo, zo, i) + hd]

    def share(act, xo, zo, i):
        s = source(xo, zo, i)
        part = kv.at[2 * s + hd]
        act(remote(part, part, sd.at[s], rd.at[s], me, other))

    x_left, x_right, x_far = (x + 3) % 4, (x + 1) % 4, (x + 2) % 4

    def relay(act, between=None):
        waiting = act is go
        for i in ARRIVAL:
            part = piece_of(x, z, i)
            if waiting:
                landed(part.at[0], ru.at[i, 0])
                landed(part.at[1], ru.at[i, 1])
            act(remote(part, part, s_own.at[i, 0], rx.at[0, 0, i], right, hd))
            act(remote(part, part, s_own.at[i, 1], rx.at[1, 0, i], left, hd))
            act(remote(part, part, s_own.at[i, 2], rz.at[0, i], across, hd))
            share(act, x, z, i)
        for i in ARRIVAL:
            if i in EARLY:
                part = piece_of(x, zp, i)
                if waiting:
                    landed(part, rz.at[0, i])
                act(remote(part, part, s_far.at[i, 0], rx.at[0, 1, i], right, hd))
                act(remote(part, part, s_far.at[i, 1], rx.at[1, 1, i], left, hd))
                share(act, x, zp, i)
        for zrel, zo in ((0, z), (1, zp)):
            for i in ARRIVAL:
                if zrel and i not in EARLY:
                    continue
                for side, xo, onward, half in ((0, x_left, right, 0), (1, x_right, left, 1)):
                    part = piece_of(xo, zo, i)
                    if waiting:
                        landed(part, rx.at[side, zrel, i])
                    act(remote(part.at[half], part.at[half], s_half.at[side, zrel, i],
                               rx.at[2 + side, zrel, i], onward, hd))
                    if i not in EARLY:
                        act(remote(part, part, s_z.at[side, i], rz.at[1 + side, i], across, hd))
                    share(act, xo, zo, i)
        if waiting:
            between()
        for zrel, zo in ((0, z), (1, zp)):
            for i in ARRIVAL:
                if zrel and i not in EARLY:
                    continue
                part = piece_of(x_far, zo, i)
                if waiting:
                    landed(part.at[0], rx.at[2, zrel, i])
                    landed(part.at[1], rx.at[3, zrel, i])
                if i not in EARLY:
                    act(remote(part, part, s_z.at[2, i], rz.at[3, i], across, hd))
                share(act, x_far, zo, i)
        for n, xo in enumerate((x, x_left, x_right, x_far)):
            for i in ARRIVAL:
                if i not in EARLY:
                    if waiting:
                        landed(piece_of(xo, zp, i), rz.at[n, i])
                    share(act, xo, zp, i)

    ones = jnp.ones((KEYS, WIDTH), jnp.bfloat16)

    def slot_of(i):
        return 2 * chip(x, jnp.where(i >= 4, 3 - z, z), (y + i % 4) % 4) + hd

    def queries_of(i):
        whole = q_buf[i]
        return jnp.concatenate([whole[:, g * WIDTH:(g + 1) * WIDTH] for g in range(GROUP)], axis=0)

    def score(q, keys):
        return lax.dot_general(q, keys, (((1,), (1,)), ((), ())), preferred_element_type=jnp.float32)

    def own(i, carry):
        landed(q_buf.at[i], rq.at[i])
        slot = slot_of(i)
        begin = span_ref[slot] * SPAN
        row = lax.broadcasted_iota(jnp.int32, (SPAN, WIDTH), 0)
        low = jnp.zeros((SPAN, WIDTH), jnp.int32)
        for d in range(1, DOCS):
            start = index[1, d]
            low = jnp.maximum(low, jnp.where(start <= begin + row, start, 0))
        low = low - begin
        penalty[i] = jnp.where(low < 0, 0.0, -NEG)
        key = lax.broadcasted_iota(jnp.int32, (SPAN, WIDTH), 1)
        bias = jnp.where((key >= low) & (key <= row), 0.0, NEG)[:, :SPAN]
        s = score(queries_of(i), kv[slot, 0]) + jnp.concatenate([bias] * GROUP, axis=0)
        top = jnp.max(s, axis=1, keepdims=True)
        weights = jnp.exp2(s * FACTOR - top * FACTOR).astype(jnp.bfloat16)
        own_top[i] = jnp.broadcast_to(top, (ROWS, WIDTH))
        values = jnp.concatenate([kv[slot, 1], ones[:SPAN]], axis=1)
        own_acc[i] = jnp.dot(weights, values, preferred_element_type=jnp.float32)
        return carry

    def own_blocks():
        lax.fori_loop(0, PIECES, own, 0)

    table_copy.start()
    table_copy.wait()
    relay(go, own_blocks)

    def shared(s, carry):
        landed(kv.at[2 * s + other], rd.at[s])
        return carry

    lax.fori_loop(0, 64, shared, 0)

    where_key = lax.broadcasted_iota(jnp.int32, (1, KEYS), 1)
    where_key = where_key - 2 * SPAN * (where_key // SPAN)

    def give_back(act, i):
        to = chip(x, jnp.where(i >= 4, 3 - z, z), (y + i % 4) % 4)
        act(remote(o_buf.at[i], attn.at[my_rows, my_queries], so.at[i], ro.at[hd * 4 + y], to, z // 2))

    def slot_at(place):
        return jnp.clip(index[0, jnp.clip(place, 0, 127)], 0, 127)

    def attend(n, carry):
        i = jnp.int32(0)
        for k, piece in enumerate(RETURN):
            i = jnp.where(n == k, piece, i)
        slot = slot_of(i)
        c = span_ref[slot]
        begin = c * SPAN
        low = jnp.int32(0)
        for d in range(1, DOCS):
            start = index[1, d]
            low = jnp.maximum(low, jnp.where(start <= begin, start, 0))
        q = queries_of(i)
        peak = jnp.full((ROWS, WIDTH), NEG, jnp.float32)
        for j in range(STEPS):
            slots = [slot_at(c - 1 - (STEP * j + t)) for t in range(STEP)]
            keys = jnp.concatenate([kv[s, 0] for s in slots], axis=0)
            bias = jnp.where(where_key >= low - SPAN * (c - 1 - STEP * j), 0.0, NEG)
            for h in range(KEYS // 256):
                cut = slice(h * 256, (h + 1) * 256)
                part = score(q, keys[cut]) + bias[:, cut]
                scores[:, j * KEYS + h * 256:j * KEYS + (h + 1) * 256] = part
                peak = jnp.maximum(peak, jnp.maximum(part[:, :WIDTH], part[:, WIDTH:]))
        fence = jnp.concatenate([penalty[i]] * GROUP, axis=0)
        mine = own_top[i]
        top = jnp.maximum(jnp.max(peak, axis=1, keepdims=True) - fence, mine)
        fade = jnp.exp2((mine - top) * FACTOR)
        acc = own_acc[i] * jnp.concatenate([fade, fade], axis=1)
        shift = top * FACTOR + fence
        shift = jnp.concatenate([shift] * (KEYS // WIDTH), axis=1)
        for j in range(STEPS):
            slots = [slot_at(c - 1 - (STEP * j + t)) for t in range(STEP)]
            values = jnp.concatenate([kv[s, 1] for s in slots], axis=0)
            values = jnp.concatenate([values, ones], axis=1)
            weights = jnp.exp2(scores[:, j * KEYS:(j + 1) * KEYS] * FACTOR - shift).astype(jnp.bfloat16)
            acc = acc + jnp.dot(weights, values, preferred_element_type=jnp.float32)
        result = (acc[:, :WIDTH] / acc[:, WIDTH:]).astype(jnp.bfloat16)
        for g in range(GROUP):
            o_buf[i, :, g * WIDTH:(g + 1) * WIDTH] = result[g * SPAN:(g + 1) * SPAN]
        local = home & (i == 0)

        @pl.when(local)
        def _():
            attn[my_rows, my_queries] = o_buf[0]

        @pl.when(jnp.logical_not(local))
        def _():
            give_back(go, i)

        return carry

    lax.fori_loop(0, PIECES, attend, 0)

    for k in range(2):
        for j in range(4):
            @pl.when(jnp.logical_not(home & (hd == k) & (y == j)))
            def _():
                landed(attn.at[pl.ds(k * SPAN, SPAN), pl.ds(j * GROUP * WIDTH, GROUP * WIDTH)], ro.at[k * 4 + j])

    w_load.wait()
    count, width = outgoing.shape[0], outgoing.shape[2]

    def hand_over(n):
        return remote(outgoing.at[n], incoming.at[n], xs.at[n], xr.at[n], me, other)

    @pl.loop(0, count)
    def _(n):
        columns = pl.ds(pl.multiple_of(n * width, width), width)
        product = jnp.dot(attn[...], w_vmem[:, columns], preferred_element_type=jnp.float32)
        upper, lower = product[:SPAN], product[SPAN:]
        first = hd == 0
        outgoing[n] = jnp.where(first, lower, upper).astype(jnp.bfloat16)
        kept[n] = jnp.where(first, upper, lower)
        hand_over(n).start()

    for n in range(count):
        hand_over(n).wait_recv()
        out_ref[:, n * width:(n + 1) * width] = (kept[n] + incoming[n].astype(jnp.float32)).astype(jnp.bfloat16)

    for n in range(count):
        hand_over(n).wait_send()
    scatter(sent, "kv")
    scatter(sent, "q")
    relay(sent)
    for i in range(PIECES):
        if i:
            give_back(sent, jnp.int32(i))
        else:
            pl.when(jnp.logical_not(home))(lambda: give_back(sent, jnp.int32(0)))


def local(queries, keys, values, span_table, doc_ids, out_weight):
    model = out_weight.shape[1]
    count = 8
    vmem, hbm = pltpu.VMEM, pl.ANY
    spec = lambda space: pl.BlockSpec(memory_space=space)
    dma = pltpu.SemaphoreType.DMA
    f32, bf16, i32 = jnp.float32, jnp.bfloat16, jnp.int32
    return pl.pallas_call(
        kernel,
        out_shape=jax.ShapeDtypeStruct((SPAN, model), bf16),
        in_specs=[spec(pltpu.SMEM), spec(vmem), spec(vmem), spec(hbm), spec(hbm), spec(hbm), spec(hbm)],
        out_specs=spec(vmem),
        scratch_shapes=[
            vmem(queries.shape, bf16),
            vmem(keys.shape, bf16),
            vmem(values.shape, bf16),
            vmem((128, 2, SPAN, WIDTH), bf16),
            vmem((PIECES, SPAN, GROUP * WIDTH), bf16),
            vmem((PIECES, SPAN, GROUP * WIDTH), bf16),
            vmem(queries.shape, bf16),
            vmem(out_weight.shape, bf16),
            vmem((ROWS, BACK * SPAN), f32),
            vmem((PIECES, ROWS, 2 * WIDTH), f32),
            vmem((PIECES, ROWS, WIDTH), f32),
            vmem((PIECES, SPAN, WIDTH), f32),
            vmem((8, 128), i32),
            vmem((count, SPAN, model // count), bf16),
            vmem((count, SPAN, model // count), bf16),
            vmem((count, SPAN, model // count), f32),
            pltpu.SMEM((8, 128), i32),
            dma((3,)), dma((3,)), dma, dma,
            dma((4, 2, 2)), dma((4, 2)), dma((PIECES, 2)), dma((PIECES,)),
            dma((PIECES, 3)), dma((PIECES, 2)), dma((2, 2, PIECES)), dma((3, PIECES)),
            dma((4, 2, PIECES)), dma((4, PIECES)), dma((64,)), dma((64,)),
            dma((PIECES,)), dma((PIECES,)), dma((count,)), dma((count,)),
        ],
        compiler_params=pltpu.CompilerParams(
            collective_id=0, has_side_effects=True, vmem_limit_bytes=60 * 2 ** 20,
        ),
    )(span_table, span_table.reshape(1, 128), doc_ids.reshape(-1, 128), queries, keys, values, out_weight)


def solution(mesh):
    return jax.shard_map(
        local,
        mesh=mesh,
        in_specs=(P("cp", "hd"), P("cp", "hd"), P("cp", "hd"), P(), P(), P("hd", None)),
        out_specs=P(("cp", "hd"), None),
        check_vma=False,
    )
```

time: 378 us -> 74.9 us (0.20)
  the two profiles are of different devices: /device:TPU:5 before, /device:TPU:65 now
where the time goes in v1:
time: 74.9 us; the launch traced here: 74.7 us
  Pallas kernels  72.7 us (97%)
  local copies, waits for them, and re-layouts  2.06 us (3%)
    pallas_call x1, Pallas kernels, local(): pl.pallas_call(kernel, out_shape=jax.ShapeDtypeStruct((SPAN, model), bf16...  72.7 us
    unnamed x1, local copies, waits for them, and re-layouts  2.06 us

profile of v1, /device:TPU:65, one launch (start us, length us, event | category | flops | bytes accessed | tf_op | source)
XLA Modules:
  0.0 74.7 jit_solution(1209993926473944286)
XLA Ops:
  0.0 72.7 %shard_map.64 = bf16[96,4096]{1,0:T(8,128)(2,1)} custom-call(s32[128]{0:T(128)} %span_ref.1, s32[1,128]{1,0:T(1,128)} %bitcast.3, s32[96,128]{1,0:T(8,128)} %bitcast.2, bf16[192,2048]{1,0:T(8,128)(2,1)} %q_hbm.1, bf16[192,512]{1,0:T(8,128)(2,1)} %k_hbm.1, bf16[192,512]{1,0:T(8,128)(2,1)} %v_hbm.1, bf16[2048,4096]{1,0:T(8,128)(2,1)} %w_hbm.1), custom_call_target="tpu_custom_call" | custom-call | tf_op jit(solution)/shard_map/pallas_call | solution.py:364
  72.7 2.1 %copy.8 = bf16[96,4096]{1,0:T(8,128)(2,1)} copy(bf16[96,4096]{1,0:T(8,128)(2,1)} %shard_map.64) | data formatting | bytes 1572864

commit v2 on v1

--- a/solution.py
+++ b/solution.py
@@ -17,20 +17,21 @@
 BACK = 32
 STEP = 8
 KEYS = STEP * SPAN
-STEPS = BACK // STEP
+BLOCKS = BACK * SPAN // 256
 NEG = -1e30
 MESH = pl.DeviceIdType.MESH
 FACTOR = WIDTH ** -0.5 * math.log2(math.e)
 ARRIVAL = (0, 1, 3, 4, 2, 5, 7, 6)
-EARLY = (0, 1, 3, 4, 2)
+EARLY = (0, 1, 3, 4)
+SPLIT = 2
 RETURN = (6, 5, 7, 2, 4, 1, 3, 0)
 
 
 def kernel(
-    span_ref, span_row_ref, doc_ref, q_hbm, k_hbm, v_hbm, w_hbm, out_ref,
-    q_in, k_in, v_in, kv, q_buf, o_buf, attn, w_vmem, scores, own_acc, own_top, penalty, table,
-    outgoing, incoming, kept, index,
-    load_sem, local_sem, w_sem, table_sem,
+    span_hbm, span_row_hbm, doc_hbm, q_hbm, k_hbm, v_hbm, w_hbm, out_ref,
+    q_in, k_in, v_in, kv, q_buf, o_buf, attn, w_vmem, scores0, scores1, shift0, shift1, fade0, fade1, peak, place_of, own_acc, own_top, penalty, table,
+    outgoing, incoming, kept, result_of, span_row_ref, doc_ref, span_ref, index,
+    load_sem, small_sem, w_sem, table_sem, out_sem,
     su, sq, ru, rq, s_own, s_far, s_half, s_z, rx, rz, sd, rd, so, ro, xs, xr,
 ):
     me = lax.axis_index("cp")
@@ -78,7 +79,12 @@
         pltpu.make_async_copy(q_hbm.at[my_rows, my_queries], q_buf.at[0], rq.at[0]),
     ]
     w_load = pltpu.make_async_copy(w_hbm, w_vmem, w_sem)
-    for load in loads:
+    small = [
+        pltpu.make_async_copy(span_row_hbm, span_row_ref, small_sem.at[0]),
+        pltpu.make_async_copy(doc_hbm, doc_ref, small_sem.at[1]),
+        pltpu.make_async_copy(span_hbm, span_ref, small_sem.at[2]),
+    ]
+    for load in loads + small:
         load.start()
 
     barrier = pltpu.get_barrier_semaphore()
@@ -93,6 +99,8 @@
     for target in (right, left, across):
         greet(target, hd)
 
+    for load in small:
+        load.wait()
     spans = jnp.broadcast_to(span_row_ref[...].astype(jnp.float32), (128, 128)).T
     held_by = lax.broadcasted_iota(jnp.int32, (128, 128), 0).astype(jnp.float32)
     wanted = lax.broadcasted_iota(jnp.int32, (128, 128), 1).astype(jnp.float32)
@@ -156,6 +164,18 @@
 
     x_left, x_right, x_far = (x + 3) % 4, (x + 1) % 4, (x + 2) % 4
 
+    def if_early(i, fn):
+        if i == SPLIT:
+            pl.when(hd == 0)(fn)
+        elif i in EARLY:
+            fn()
+
+    def if_late(i, fn):
+        if i == SPLIT:
+            pl.when(hd == 1)(fn)
+        elif i not in EARLY:
+            fn()
+
     def relay(act, between=None):
         waiting = act is go
         for i in ARRIVAL:
@@ -167,51 +187,60 @@
             act(remote(part, part, s_own.at[i, 1], rx.at[1, 0, i], left, hd))
             act(remote(part, part, s_own.at[i, 2], rz.at[0, i], across, hd))
             share(act, x, z, i)
-        for i in ARRIVAL:
-            if i in EARLY:
-                part = piece_of(x, zp, i)
+
+        def from_across(i):
+            part = piece_of(x, zp, i)
+            if waiting:
+                landed(part, rz.at[0, i])
+            act(remote(part, part, s_far.at[i, 0], rx.at[0, 1, i], right, hd))
+            act(remote(part, part, s_far.at[i, 1], rx.at[1, 1, i], left, hd))
+            share(act, x, zp, i)
+
+        def from_side(i, zrel, zo):
+            for side, xo, onward, half in ((0, x_left, right, 0), (1, x_right, left, 1)):
+                part = piece_of(xo, zo, i)
                 if waiting:
-                    landed(part, rz.at[0, i])
-                act(remote(part, part, s_far.at[i, 0], rx.at[0, 1, i], right, hd))
-                act(remote(part, part, s_far.at[i, 1], rx.at[1, 1, i], left, hd))
-                share(act, x, zp, i)
-        for zrel, zo in ((0, z), (1, zp)):
-            for i in ARRIVAL:
-                if zrel and i not in EARLY:
-                    continue
-                for side, xo, onward, half in ((0, x_left, right, 0), (1, x_right, left, 1)):
-                    part = piece_of(xo, zo, i)
-                    if waiting:
-                        landed(part, rx.at[side, zrel, i])
-                    act(remote(part.at[half], part.at[half], s_half.at[side, zrel, i],
-                               rx.at[2 + side, zrel, i], onward, hd))
-                    if i not in EARLY:
-                        act(remote(part, part, s_z.at[side, i], rz.at[1 + side, i], across, hd))
-                    share(act, xo, zo, i)
-        if waiting:
-            between()
-        for zrel, zo in ((0, z), (1, zp)):
-            for i in ARRIVAL:
-                if zrel and i not in EARLY:
-                    continue
-                part = piece_of(x_far, zo, i)
-                if waiting:
-                    landed(part.at[0], rx.at[2, zrel, i])
-                    landed(part.at[1], rx.at[3, zrel, i])
-                if i not in EARLY:
-                    act(remote(part, part, s_z.at[2, i], rz.at[3, i], across, hd))
-                share(act, x_far, zo, i)
+                    landed(part, rx.at[side, zrel, i])
+                act(remote(part.at[half], part.at[half], s_half.at[side, zrel, i],
+                           rx.at[2 + side, zrel, i], onward, hd))
+                if not zrel:
+                    if_late(i, lambda: act(remote(part, part, s_z.at[side, i], rz.at[1 + side, i], across, hd)))
+                share(act, xo, zo, i)
+
+        def from_far(i, zrel, zo):
+            part = piece_of(x_far, zo, i)
+            if waiting:
+                landed(part.at[0], rx.at[2, zrel, i])
+                landed(part.at[1], rx.at[3, zrel, i])
+            if not zrel:
+                if_late(i, lambda: act(remote(part, part, s_z.at[2, i], rz.at[3, i], across, hd)))
+            share(act, x_far, zo, i)
+
+        def last(i, n, xo):
+            if waiting:
+                landed(piece_of(xo, zp, i), rz.at[n, i])
+            share(act, xo, zp, i)
+
+        for i in ARRIVAL:
+            if_early(i, lambda: from_across(i))
+        for i in ARRIVAL:
+            from_side(i, 0, z)
+        for i in ARRIVAL:
+            if_early(i, lambda: from_side(i, 1, zp))
+        for i in ARRIVAL:
+            from_far(i, 0, z)
+            if waiting:
+                between(i)
+        for i in ARRIVAL:
+            if_early(i, lambda: from_far(i, 1, zp))
         for n, xo in enumerate((x, x_left, x_right, x_far)):
             for i in ARRIVAL:
-                if i not in EARLY:
-                    if waiting:
-                        landed(piece_of(xo, zp, i), rz.at[n, i])
-                    share(act, xo, zp, i)
+                if_late(i, lambda: last(i, n, xo))
 
     ones = jnp.ones((KEYS, WIDTH), jnp.bfloat16)
 
     def slot_of(i):
-        return 2 * chip(x, jnp.where(i >= 4, 3 - z, z), (y + i % 4) % 4) + hd
+        return 2 * chip(x, jnp.where(jnp.int32(i) >= 4, 3 - z, z), (y + i % 4) % 4) + hd
 
     def queries_of(i):
         whole = q_buf[i]
@@ -220,7 +249,7 @@
     def score(q, keys):
         return lax.dot_general(q, keys, (((1,), (1,)), ((), ())), preferred_element_type=jnp.float32)
 
-    def own(i, carry):
+    def own(i):
         landed(q_buf.at[i], rq.at[i])
         slot = slot_of(i)
         begin = span_ref[slot] * SPAN
@@ -239,14 +268,12 @@
         own_top[i] = jnp.broadcast_to(top, (ROWS, WIDTH))
         values = jnp.concatenate([kv[slot, 1], ones[:SPAN]], axis=1)
         own_acc[i] = jnp.dot(weights, values, preferred_element_type=jnp.float32)
-        return carry
-
-    def own_blocks():
-        lax.fori_loop(0, PIECES, own, 0)
 
     table_copy.start()
     table_copy.wait()
-    relay(go, own_blocks)
+    place = lax.broadcasted_iota(jnp.int32, (1, BACK * SPAN), 1)
+    place_of[...] = place - 2 * SPAN * (place // SPAN)
+    relay(go, own)
 
     def shared(s, carry):
         landed(kv.at[2 * s + other], rd.at[s])
@@ -254,9 +281,6 @@
 
     lax.fori_loop(0, 64, shared, 0)
 
-    where_key = lax.broadcasted_iota(jnp.int32, (1, KEYS), 1)
-    where_key = where_key - 2 * SPAN * (where_key // SPAN)
-
     def give_back(act, i):
         to = chip(x, jnp.where(i >= 4, 3 - z, z), (y + i % 4) % 4)
         act(remote(o_buf.at[i], attn.at[my_rows, my_queries], so.at[i], ro.at[hd * 4 + y], to, z // 2))
@@ -264,57 +288,96 @@
     def slot_at(place):
         return jnp.clip(index[0, jnp.clip(place, 0, 127)], 0, 127)
 
-    def attend(n, carry):
+    def block_of(c, t, which):
+        parts = []
+        for tile in range(256 * t // SPAN, (256 * t + 255) // SPAN + 1):
+            first, last = max(256 * t - SPAN * tile, 0), min(256 * t + 256 - SPAN * tile, SPAN)
+            parts.append(kv[slot_at(c - 1 - tile), which, first:last])
+        return jnp.concatenate(parts, axis=0)
+
+    def turn(n):
         i = jnp.int32(0)
         for k, piece in enumerate(RETURN):
             i = jnp.where(n == k, piece, i)
-        slot = slot_of(i)
-        c = span_ref[slot]
-        begin = c * SPAN
-        low = jnp.int32(0)
-        for d in range(1, DOCS):
-            start = index[1, d]
-            low = jnp.maximum(low, jnp.where(start <= begin, start, 0))
-        q = queries_of(i)
-        peak = jnp.full((ROWS, WIDTH), NEG, jnp.float32)
-        for j in range(STEPS):
-            slots = [slot_at(c - 1 - (STEP * j + t)) for t in range(STEP)]
-            keys = jnp.concatenate([kv[s, 0] for s in slots], axis=0)
-            bias = jnp.where(where_key >= low - SPAN * (c - 1 - STEP * j), 0.0, NEG)
-            for h in range(KEYS // 256):
-                cut = slice(h * 256, (h + 1) * 256)
-                part = score(q, keys[cut]) + bias[:, cut]
-                scores[:, j * KEYS + h * 256:j * KEYS + (h + 1) * 256] = part
-                peak = jnp.maximum(peak, jnp.maximum(part[:, :WIDTH], part[:, WIDTH:]))
-        fence = jnp.concatenate([penalty[i]] * GROUP, axis=0)
-        mine = own_top[i]
-        top = jnp.maximum(jnp.max(peak, axis=1, keepdims=True) - fence, mine)
-        fade = jnp.exp2((mine - top) * FACTOR)
-        acc = own_acc[i] * jnp.concatenate([fade, fade], axis=1)
-        shift = top * FACTOR + fence
-        shift = jnp.concatenate([shift] * (KEYS // WIDTH), axis=1)
-        for j in range(STEPS):
-            slots = [slot_at(c - 1 - (STEP * j + t)) for t in range(STEP)]
-            values = jnp.concatenate([kv[s, 1] for s in slots], axis=0)
-            values = jnp.concatenate([values, ones], axis=1)
-            weights = jnp.exp2(scores[:, j * KEYS:(j + 1) * KEYS] * FACTOR - shift).astype(jnp.bfloat16)
-            acc = acc + jnp.dot(weights, values, preferred_element_type=jnp.float32)
-        result = (acc[:, :WIDTH] / acc[:, WIDTH:]).astype(jnp.bfloat16)
-        for g in range(GROUP):
-            o_buf[i, :, g * WIDTH:(g + 1) * WIDTH] = result[g * SPAN:(g + 1) * SPAN]
-        local = home & (i == 0)
-
-        @pl.when(local)
-        def _():
-            attn[my_rows, my_queries] = o_buf[0]
-
-        @pl.when(jnp.logical_not(local))
-        def _():
-            give_back(go, i)
-
+        return i
+
+    def stage(ahead, now):
+        if ahead is not None:
+            n, s_a, shift_a, fade_a = ahead
+            i = turn(n)
+            c = span_ref[slot_of(i)]
+            begin = c * SPAN
+            low = jnp.int32(0)
+            for d in range(1, DOCS):
+                start = index[1, d]
+                low = jnp.maximum(low, jnp.where(start <= begin, start, 0))
+            q = queries_of(i)
+            reach = low - (begin - SPAN)
+            done = 0
+        if now is not None:
+            nb, s_b, shift_b, fade_b = now
+            ib = turn(nb)
+            cb = span_ref[slot_of(ib)]
+            acc = None
+
+        def raise_peak(t):
+            top = s_a[:, t * KEYS:t * KEYS + WIDTH]
+            for l in range(1, KEYS // WIDTH):
+                top = jnp.maximum(top, s_a[:, t * KEYS + l * WIDTH:t * KEYS + (l + 1) * WIDTH])
+            peak[...] = top if t == 0 else jnp.maximum(peak[...], top)
+
+        for t in range(BLOCKS):
+            cut = slice(t * 256, (t + 1) * 256)
+            if ahead is not None:
+                bias = jnp.where(place_of[:, cut] >= reach, 0.0, NEG)
+                s_a[:, cut] = score(q, block_of(c, t, 0)) + bias
+                if t >= 4 and (t - 4) % 3 == 0:
+                    raise_peak((t - 4) // 3)
+            if now is not None:
+                shift = shift_b[...]
+                shift = jnp.concatenate([shift, shift], axis=1)
+                weights = jnp.exp2(s_b[:, cut] * FACTOR - shift).astype(jnp.bfloat16)
+                values = jnp.concatenate([block_of(cb, t, 1), ones[:256]], axis=1)
+                cuts = (slice(0, ROWS),) if ahead is not None else (slice(0, ROWS // 2), slice(ROWS // 2, ROWS))
+                parts = [jnp.dot(weights[r], values, preferred_element_type=jnp.float32) for r in cuts]
+                acc = parts if acc is None else [a + b for a, b in zip(acc, parts)]
+        if ahead is not None:
+            raise_peak(BLOCKS // 3 - 1)
+            fence = jnp.concatenate([penalty[i]] * GROUP, axis=0)
+            mine = own_top[i]
+            top = jnp.maximum(jnp.max(peak[...], axis=1, keepdims=True) - fence, mine)
+            fade_a[...] = jnp.exp2((mine - top) * FACTOR)
+            shift_a[...] = top * FACTOR + fence
+        if now is not None:
+            fade = fade_b[...]
+            acc = jnp.concatenate(acc, axis=0) + own_acc[ib] * jnp.concatenate([fade, fade], axis=1)
+            result = (acc[:, :WIDTH] / acc[:, WIDTH:]).astype(jnp.bfloat16)
+            for g in range(GROUP):
+                o_buf[ib, :, g * WIDTH:(g + 1) * WIDTH] = result[g * SPAN:(g + 1) * SPAN]
+
+    even = (scores0, shift0, fade0)
+    odd = (scores1, shift1, fade1)
+    stage((jnp.int32(0),) + even, None)
+
+    def pair(k, carry):
+        stage((2 * k + 1,) + odd, (2 * k,) + even)
+        give_back(go, turn(2 * k))
+        stage((2 * k + 2,) + even, (2 * k + 1,) + odd)
+        give_back(go, turn(2 * k + 1))
         return carry
 
-    lax.fori_loop(0, PIECES, attend, 0)
+    lax.fori_loop(0, PIECES // 2 - 1, pair, 0)
+    stage((jnp.int32(PIECES - 1),) + odd, (jnp.int32(PIECES - 2),) + even)
+    give_back(go, jnp.int32(RETURN[PIECES - 2]))
+    stage(None, (jnp.int32(PIECES - 1),) + odd)
+
+    @pl.when(home)
+    def _():
+        attn[my_rows, my_queries] = o_buf[0]
+
+    @pl.when(jnp.logical_not(home))
+    def _():
+        give_back(go, jnp.int32(0))
 
     for k in range(2):
         for j in range(4):
@@ -338,12 +401,16 @@
         kept[n] = jnp.where(first, upper, lower)
         hand_over(n).start()
 
+    def put(n):
+        return pltpu.make_async_copy(result_of.at[n], out_ref.at[:, pl.ds(n * width, width)], out_sem.at[n])
+
     for n in range(count):
         hand_over(n).wait_recv()
-        out_ref[:, n * width:(n + 1) * width] = (kept[n] + incoming[n].astype(jnp.float32)).astype(jnp.bfloat16)
-
-    for n in range(count):
-        hand_over(n).wait_send()
+        result_of[n] = (kept[n] + incoming[n].astype(jnp.float32)).astype(jnp.bfloat16)
+        if n:
+            put(n - 1).start()
+
+    put(count - 1).start()
     scatter(sent, "kv")
     scatter(sent, "q")
     relay(sent)
@@ -352,6 +419,9 @@
             give_back(sent, jnp.int32(i))
         else:
             pl.when(jnp.logical_not(home))(lambda: give_back(sent, jnp.int32(0)))
+    for n in range(count):
+        hand_over(n).wait_send()
+        put(n).wait()
 
 
 def local(queries, keys, values, span_table, doc_ids, out_weight):
@@ -364,8 +434,8 @@
     return pl.pallas_call(
         kernel,
         out_shape=jax.ShapeDtypeStruct((SPAN, model), bf16),
-        in_specs=[spec(pltpu.SMEM), spec(vmem), spec(vmem), spec(hbm), spec(hbm), spec(hbm), spec(hbm)],
-        out_specs=spec(vmem),
+        in_specs=[spec(hbm)] * 7,
+        out_specs=spec(hbm),
         scratch_shapes=[
             vmem(queries.shape, bf16),
             vmem(keys.shape, bf16),
@@ -376,6 +446,13 @@
             vmem(queries.shape, bf16),
             vmem(out_weight.shape, bf16),
             vmem((ROWS, BACK * SPAN), f32),
+            vmem((ROWS, BACK * SPAN), f32),
+            vmem((ROWS, WIDTH), f32),
+            vmem((ROWS, WIDTH), f32),
+            vmem((ROWS, WIDTH), f32),
+            vmem((ROWS, WIDTH), f32),
+            vmem((ROWS, WIDTH), f32),
+            vmem((1, BACK * SPAN), i32),
             vmem((PIECES, ROWS, 2 * WIDTH), f32),
             vmem((PIECES, ROWS, WIDTH), f32),
             vmem((PIECES, SPAN, WIDTH), f32),
@@ -383,8 +460,12 @@
             vmem((count, SPAN, model // count), bf16),
             vmem((count, SPAN, model // count), bf16),
             vmem((count, SPAN, model // count), f32),
+            vmem((count, SPAN, model // count), bf16),
+            vmem((1, 128), i32),
+            vmem((doc_ids.shape[0] // 128, 128), i32),
+            pltpu.SMEM((128,), i32),
             pltpu.SMEM((8, 128), i32),
-            dma((3,)), dma((3,)), dma, dma,
+            dma((3,)), dma((3,)), dma, dma, dma((count,)),
             dma((4, 2, 2)), dma((4, 2)), dma((PIECES, 2)), dma((PIECES,)),
             dma((PIECES, 3)), dma((PIECES, 2)), dma((2, 2, PIECES)), dma((3, PIECES)),
             dma((4, 2, PIECES)), dma((4, PIECES)), dma((64,)), dma((64,)),

time: 74.9 us -> 64.9 us (0.87)
  the two profiles are of different devices: /device:TPU:65 before, /device:TPU:17 now
where the time goes in v2:
time: 64.9 us; the launch traced here: 63.9 us
  Pallas kernels  61.8 us (95%)
  local copies, waits for them, and re-layouts  2.06 us (3%)
    pallas_call x1, Pallas kernels, local(): pl.pallas_call(kernel, out_shape=jax.ShapeDtypeStruct((SPAN, model), bf16...  61.8 us
    unnamed x1, local copies, waits for them, and re-layouts  2.06 us

profile of v2, /device:TPU:17, one launch (start us, length us, event | category | flops | bytes accessed | tf_op | source)
XLA Modules:
  0.0 63.9 jit_solution(341660221583457161)
XLA Ops:
  0.0 61.8 %shard_map.64 = bf16[96,4096]{1,0:T(8,128)(2,1)} custom-call(s32[128]{0:T(128)} %span_hbm.1, s32[1,128]{1,0:T(1,128)} %bitcast.3, s32[96,128]{1,0:T(8,128)} %bitcast.2, bf16[192,2048]{1,0:T(8,128)(2,1)} %q_hbm.1, bf16[192,512]{1,0:T(8,128)(2,1)} %k_hbm.1, bf16[192,512]{1,0:T(8,128)(2,1)} %v_hbm.1, bf16[2048,4096]{1,0:T(8,128)(2,1)} %w_hbm.1), custom_call_target="tpu_custom_call" | custom-call | tf_op jit(solution)/shard_map/pallas_call | solution.py:434
  61.8 2.1 %copy.8 = bf16[96,4096]{1,0:T(8,128)(2,1)} copy(bf16[96,4096]{1,0:T(8,128)(2,1)} %shard_map.64) | data formatting | bytes 1572864

commit v3 on v2

--- a/solution.py
+++ b/solution.py
@@ -22,9 +22,10 @@
 MESH = pl.DeviceIdType.MESH
 FACTOR = WIDTH ** -0.5 * math.log2(math.e)
 ARRIVAL = (0, 1, 3, 4, 2, 5, 7, 6)
-EARLY = (0, 1, 3, 4)
-SPLIT = 2
-RETURN = (6, 5, 7, 2, 4, 1, 3, 0)
+EARLY = (2, 5, 7, 6)
+LATE = (0, 1, 3)
+SPLIT = 4
+RETURN = (6, 5, 2, 7, 1, 4, 3, 0)
 
 
 def kernel(
@@ -87,6 +88,11 @@
     for load in loads + small:
         load.start()
 
+    @pl.when(home)
+    def _():
+        for copy in locals_:
+            copy.start()
+
     barrier = pltpu.get_barrier_semaphore()
 
     def greet(cp, core):
@@ -141,11 +147,6 @@
                 else:
                     one()
 
-    @pl.when(home)
-    def _():
-        for copy in locals_:
-            copy.start()
-
     loads[0].wait()
     loads[1].wait()
     scatter(go, "kv")
@@ -160,7 +161,7 @@
     def share(act, xo, zo, i):
         s = source(xo, zo, i)
         part = kv.at[2 * s + hd]
-        act(remote(part, part, sd.at[s], rd.at[s], me, other))
+        act(remote(part, part, sd.at[s], rd, me, other))
 
     x_left, x_right, x_far = (x + 3) % 4, (x + 1) % 4, (x + 2) % 4
 
@@ -173,7 +174,7 @@
     def if_late(i, fn):
         if i == SPLIT:
             pl.when(hd == 1)(fn)
-        elif i not in EARLY:
+        elif i in LATE:
             fn()
 
     def relay(act, between=None):
@@ -221,21 +222,32 @@
                 landed(piece_of(xo, zp, i), rz.at[n, i])
             share(act, xo, zp, i)
 
-        for i in ARRIVAL:
+        def extra(k):
+            if waiting:
+                between(ARRIVAL[k])
+
+        near = LATE + (SPLIT,)
+        for i in near:
+            if_late(i, lambda: from_side(i, 0, z))
+        for i in (SPLIT,) + EARLY:
             if_early(i, lambda: from_across(i))
-        for i in ARRIVAL:
-            from_side(i, 0, z)
-        for i in ARRIVAL:
+        for i in near:
+            if_late(i, lambda: from_far(i, 0, z))
+        for i in (SPLIT,) + EARLY:
+            if_early(i, lambda: from_side(i, 0, z))
+        for k, i in enumerate((SPLIT,) + EARLY):
             if_early(i, lambda: from_side(i, 1, zp))
-        for i in ARRIVAL:
-            from_far(i, 0, z)
-            if waiting:
-                between(i)
-        for i in ARRIVAL:
+            if k:
+                extra(k - 1)
+        for k, i in enumerate((SPLIT,) + EARLY):
+            if_early(i, lambda: from_far(i, 0, z))
+            if k:
+                extra(k + 3)
+        for n, xo in enumerate((x, x_left, x_right, x_far)):
+            for i in near:
+                if_late(i, lambda: last(i, n, xo))
+        for i in (SPLIT,) + EARLY:
             if_early(i, lambda: from_far(i, 1, zp))
-        for n, xo in enumerate((x, x_left, x_right, x_far)):
-            for i in ARRIVAL:
-                if_late(i, lambda: last(i, n, xo))
 
     ones = jnp.ones((KEYS, WIDTH), jnp.bfloat16)
 
@@ -275,11 +287,7 @@
     place_of[...] = place - 2 * SPAN * (place // SPAN)
     relay(go, own)
 
-    def shared(s, carry):
-        landed(kv.at[2 * s + other], rd.at[s])
-        return carry
-
-    lax.fori_loop(0, 64, shared, 0)
+    landed(kv.at[pl.ds(0, 64)], rd)
 
     def give_back(act, i):
         to = chip(x, jnp.where(i >= 4, 3 - z, z), (y + i % 4) % 4)
@@ -318,7 +326,7 @@
             nb, s_b, shift_b, fade_b = now
             ib = turn(nb)
             cb = span_ref[slot_of(ib)]
-            acc = None
+            acc = {}
 
         def raise_peak(t):
             top = s_a[:, t * KEYS:t * KEYS + WIDTH]
@@ -338,9 +346,9 @@
                 shift = jnp.concatenate([shift, shift], axis=1)
                 weights = jnp.exp2(s_b[:, cut] * FACTOR - shift).astype(jnp.bfloat16)
                 values = jnp.concatenate([block_of(cb, t, 1), ones[:256]], axis=1)
-                cuts = (slice(0, ROWS),) if ahead is not None else (slice(0, ROWS // 2), slice(ROWS // 2, ROWS))
-                parts = [jnp.dot(weights[r], values, preferred_element_type=jnp.float32) for r in cuts]
-                acc = parts if acc is None else [a + b for a, b in zip(acc, parts)]
+                part = jnp.dot(weights, values, preferred_element_type=jnp.float32)
+                chain = 0 if ahead is not None else t % 2
+                acc[chain] = acc[chain] + part if chain in acc else part
         if ahead is not None:
             raise_peak(BLOCKS // 3 - 1)
             fence = jnp.concatenate([penalty[i]] * GROUP, axis=0)
@@ -350,7 +358,10 @@
             shift_a[...] = top * FACTOR + fence
         if now is not None:
             fade = fade_b[...]
-            acc = jnp.concatenate(acc, axis=0) + own_acc[ib] * jnp.concatenate([fade, fade], axis=1)
+            if 1 in acc:
+                scores0[:, :2 * WIDTH] = acc[0]
+                acc = {0: acc[1] + scores0[:, :2 * WIDTH]}
+            acc = acc[0] + own_acc[ib] * jnp.concatenate([fade, fade], axis=1)
             result = (acc[:, :WIDTH] / acc[:, WIDTH:]).astype(jnp.bfloat16)
             for g in range(GROUP):
                 o_buf[ib, :, g * WIDTH:(g + 1) * WIDTH] = result[g * SPAN:(g + 1) * SPAN]
@@ -368,7 +379,7 @@
 
     lax.fori_loop(0, PIECES // 2 - 1, pair, 0)
     stage((jnp.int32(PIECES - 1),) + odd, (jnp.int32(PIECES - 2),) + even)
-    give_back(go, jnp.int32(RETURN[PIECES - 2]))
+    give_back(go, turn(jnp.int32(PIECES - 2)))
     stage(None, (jnp.int32(PIECES - 1),) + odd)
 
     @pl.when(home)
@@ -378,6 +389,10 @@
     @pl.when(jnp.logical_not(home))
     def _():
         give_back(go, jnp.int32(0))
+
+    scatter(sent, "kv")
+    scatter(sent, "q")
+    relay(sent)
 
     for k in range(2):
         for j in range(4):
@@ -401,6 +416,12 @@
         kept[n] = jnp.where(first, upper, lower)
         hand_over(n).start()
 
+    for i in range(PIECES):
+        if i:
+            give_back(sent, jnp.int32(i))
+        else:
+            pl.when(jnp.logical_not(home))(lambda: give_back(sent, jnp.int32(0)))
+
     def put(n):
         return pltpu.make_async_copy(result_of.at[n], out_ref.at[:, pl.ds(n * width, width)], out_sem.at[n])
 
@@ -411,14 +432,6 @@
             put(n - 1).start()
 
     put(count - 1).start()
-    scatter(sent, "kv")
-    scatter(sent, "q")
-    relay(sent)
-    for i in range(PIECES):
-        if i:
-            give_back(sent, jnp.int32(i))
-        else:
-            pl.when(jnp.logical_not(home))(lambda: give_back(sent, jnp.int32(0)))
     for n in range(count):
         hand_over(n).wait_send()
         put(n).wait()
@@ -468,7 +481,7 @@
             dma((3,)), dma((3,)), dma, dma, dma((count,)),
             dma((4, 2, 2)), dma((4, 2)), dma((PIECES, 2)), dma((PIECES,)),
             dma((PIECES, 3)), dma((PIECES, 2)), dma((2, 2, PIECES)), dma((3, PIECES)),
-            dma((4, 2, PIECES)), dma((4, PIECES)), dma((64,)), dma((64,)),
+            dma((4, 2, PIECES)), dma((4, PIECES)), dma((64,)), dma,
             dma((PIECES,)), dma((PIECES,)), dma((count,)), dma((count,)),
         ],
         compiler_params=pltpu.CompilerParams(

time: 64.9 us -> 62.8 us (0.968)
  Pallas kernels: 61.8 us -> 60.3 us
    pallas_call x1, Pallas kernels: 61.8 us -> 60.3 us  [local(): pl.pallas_call(kernel, out_shape=jax.ShapeDtypeStruct((SPAN, model), bf16...]
where the time goes in v3:
time: 62.8 us; the launch traced here: 62.4 us
  Pallas kernels  60.3 us (96%)
  local copies, waits for them, and re-layouts  2.06 us (3%)
    pallas_call x1, Pallas kernels, local(): pl.pallas_call(kernel, out_shape=jax.ShapeDtypeStruct((SPAN, model), bf16...  60.3 us
    unnamed x1, local copies, waits for them, and re-layouts  2.06 us

profile of v3, /device:TPU:17, one launch (start us, length us, event | category | flops | bytes accessed | tf_op | source)
XLA Modules:
  0.0 62.4 jit_solution(5541653078336468609)
XLA Ops:
  0.0 60.3 %shard_map.64 = bf16[96,4096]{1,0:T(8,128)(2,1)} custom-call(s32[128]{0:T(128)} %span_hbm.1, s32[1,128]{1,0:T(1,128)} %bitcast.3, s32[96,128]{1,0:T(8,128)} %bitcast.2, bf16[192,2048]{1,0:T(8,128)(2,1)} %q_hbm.1, bf16[192,512]{1,0:T(8,128)(2,1)} %k_hbm.1, bf16[192,512]{1,0:T(8,128)(2,1)} %v_hbm.1, bf16[2048,4096]{1,0:T(8,128)(2,1)} %w_hbm.1), custom_call_target="tpu_custom_call" | custom-call | tf_op jit(solution)/shard_map/pallas_call | solution.py:447
  60.3 2.1 %copy.8 = bf16[96,4096]{1,0:T(8,128)(2,1)} copy(bf16[96,4096]{1,0:T(8,128)(2,1)} %shard_map.64) | data formatting | bytes 1572864

commit v4 on v3

--- a/solution.py
+++ b/solution.py
@@ -23,8 +23,7 @@
 FACTOR = WIDTH ** -0.5 * math.log2(math.e)
 ARRIVAL = (0, 1, 3, 4, 2, 5, 7, 6)
 EARLY = (2, 5, 7, 6)
-LATE = (0, 1, 3)
-SPLIT = 4
+LATE = (0, 1, 3, 4)
 RETURN = (6, 5, 2, 7, 1, 4, 3, 0)
 
 
@@ -165,18 +164,6 @@
 
     x_left, x_right, x_far = (x + 3) % 4, (x + 1) % 4, (x + 2) % 4
 
-    def if_early(i, fn):
-        if i == SPLIT:
-            pl.when(hd == 0)(fn)
-        elif i in EARLY:
-            fn()
-
-    def if_late(i, fn):
-        if i == SPLIT:
-            pl.when(hd == 1)(fn)
-        elif i in LATE:
-            fn()
-
     def relay(act, between=None):
         waiting = act is go
         for i in ARRIVAL:
@@ -204,8 +191,8 @@
                     landed(part, rx.at[side, zrel, i])
                 act(remote(part.at[half], part.at[half], s_half.at[side, zrel, i],
                            rx.at[2 + side, zrel, i], onward, hd))
-                if not zrel:
-                    if_late(i, lambda: act(remote(part, part, s_z.at[side, i], rz.at[1 + side, i], across, hd)))
+                if not zrel and i in LATE:
+                    act(remote(part, part, s_z.at[side, i], rz.at[1 + side, i], across, hd))
                 share(act, xo, zo, i)
 
         def from_far(i, zrel, zo):
@@ -213,8 +200,8 @@
             if waiting:
                 landed(part.at[0], rx.at[2, zrel, i])
                 landed(part.at[1], rx.at[3, zrel, i])
-            if not zrel:
-                if_late(i, lambda: act(remote(part, part, s_z.at[2, i], rz.at[3, i], across, hd)))
+            if not zrel and i in LATE:
+                act(remote(part, part, s_z.at[2, i], rz.at[3, i], across, hd))
             share(act, x_far, zo, i)
 
         def last(i, n, xo):
@@ -226,28 +213,25 @@
             if waiting:
                 between(ARRIVAL[k])
 
-        near = LATE + (SPLIT,)
-        for i in near:
-            if_late(i, lambda: from_side(i, 0, z))
-        for i in (SPLIT,) + EARLY:
-            if_early(i, lambda: from_across(i))
-        for i in near:
-            if_late(i, lambda: from_far(i, 0, z))
-        for i in (SPLIT,) + EARLY:
-            if_early(i, lambda: from_side(i, 0, z))
-        for k, i in enumerate((SPLIT,) + EARLY):
-            if_early(i, lambda: from_side(i, 1, zp))
-            if k:
-                extra(k - 1)
-        for k, i in enumerate((SPLIT,) + EARLY):
-            if_early(i, lambda: from_far(i, 0, z))
-            if k:
-                extra(k + 3)
+        for i in LATE:
+            from_side(i, 0, z)
+        for i in EARLY:
+            from_across(i)
+        for i in LATE:
+            from_far(i, 0, z)
+        for i in EARLY:
+            from_side(i, 0, z)
+        for k, i in enumerate(EARLY):
+            from_side(i, 1, zp)
+            extra(k)
+        for k, i in enumerate(EARLY):
+            from_far(i, 0, z)
+            extra(k + 4)
         for n, xo in enumerate((x, x_left, x_right, x_far)):
-            for i in near:
-                if_late(i, lambda: last(i, n, xo))
-        for i in (SPLIT,) + EARLY:
-            if_early(i, lambda: from_far(i, 1, zp))
+            for i in LATE:
+                last(i, n, xo)
+        for i in EARLY:
+            from_far(i, 1, zp)
 
     ones = jnp.ones((KEYS, WIDTH), jnp.bfloat16)
 
@@ -309,7 +293,7 @@
             i = jnp.where(n == k, piece, i)
         return i
 
-    def stage(ahead, now):
+    def stage(ahead, now, before=None):
         if ahead is not None:
             n, s_a, shift_a, fade_a = ahead
             i = turn(n)
@@ -369,17 +353,17 @@
     even = (scores0, shift0, fade0)
     odd = (scores1, shift1, fade1)
     stage((jnp.int32(0),) + even, None)
+    stage((jnp.int32(1),) + odd, (jnp.int32(0),) + even)
+    give_back(go, turn(jnp.int32(0)))
 
     def pair(k, carry):
-        stage((2 * k + 1,) + odd, (2 * k,) + even)
-        give_back(go, turn(2 * k))
         stage((2 * k + 2,) + even, (2 * k + 1,) + odd)
         give_back(go, turn(2 * k + 1))
+        stage((2 * k + 3,) + odd, (2 * k + 2,) + even)
+        give_back(go, turn(2 * k + 2))
         return carry
 
     lax.fori_loop(0, PIECES // 2 - 1, pair, 0)
-    stage((jnp.int32(PIECES - 1),) + odd, (jnp.int32(PIECES - 2),) + even)
-    give_back(go, turn(jnp.int32(PIECES - 2)))
     stage(None, (jnp.int32(PIECES - 1),) + odd)
 
     @pl.when(home)

time: 62.8 us -> 62.1 us (0.989)
  no operation moved by 1% of the time
where the time goes in v4:
time: 62.1 us; the launch traced here: 61.9 us
  Pallas kernels  59.9 us (96%)
  local copies, waits for them, and re-layouts  2.06 us (3%)
    pallas_call x1, Pallas kernels, local(): pl.pallas_call(kernel, out_shape=jax.ShapeDtypeStruct((SPAN, model), bf16...  59.9 us
    unnamed x1, local copies, waits for them, and re-layouts  2.06 us

profile of v4, /device:TPU:17, one launch (start us, length us, event | category | flops | bytes accessed | tf_op | source)
XLA Modules:
  0.0 61.9 jit_solution(928554393754458180)
XLA Ops:
  0.0 59.9 %shard_map.64 = bf16[96,4096]{1,0:T(8,128)(2,1)} custom-call(s32[128]{0:T(128)} %span_hbm.1, s32[1,128]{1,0:T(1,128)} %bitcast.3, s32[96,128]{1,0:T(8,128)} %bitcast.2, bf16[192,2048]{1,0:T(8,128)(2,1)} %q_hbm.1, bf16[192,512]{1,0:T(8,128)(2,1)} %k_hbm.1, bf16[192,512]{1,0:T(8,128)(2,1)} %v_hbm.1, bf16[2048,4096]{1,0:T(8,128)(2,1)} %w_hbm.1), custom_call_target="tpu_custom_call" | custom-call | tf_op jit(solution)/shard_map/pallas_call | solution.py:431
  59.9 2.1 %copy.8 = bf16[96,4096]{1,0:T(8,128)(2,1)} copy(bf16[96,4096]{1,0:T(8,128)(2,1)} %shard_map.64) | data formatting | bytes 1572864

commit v5 on v4

--- a/solution.py
+++ b/solution.py
@@ -224,12 +224,14 @@
         for k, i in enumerate(EARLY):
             from_side(i, 1, zp)
             extra(k)
+        for n, xo in enumerate((x, x_left, x_right)):
+            for i in LATE:
+                last(i, n, xo)
         for k, i in enumerate(EARLY):
             from_far(i, 0, z)
             extra(k + 4)
-        for n, xo in enumerate((x, x_left, x_right, x_far)):
-            for i in LATE:
-                last(i, n, xo)
+        for i in LATE:
+            last(i, 3, x_far)
         for i in EARLY:
             from_far(i, 1, zp)
 

time: 62.1 us -> 61.3 us (0.987)
  Pallas kernels: 59.9 us -> 59 us
    pallas_call x1, Pallas kernels: 59.9 us -> 59 us  [local(): pl.pallas_call(kernel, out_shape=jax.ShapeDtypeStruct((SPAN, model), bf16...]
where the time goes in v5:
time: 61.3 us; the launch traced here: 61.1 us
  Pallas kernels  59 us (96%)
  local copies, waits for them, and re-layouts  2.06 us (3%)
    pallas_call x1, Pallas kernels, local(): pl.pallas_call(kernel, out_shape=jax.ShapeDtypeStruct((SPAN, model), bf16...  59 us
    unnamed x1, local copies, waits for them, and re-layouts  2.06 us

profile of v5, /device:TPU:17, one launch (start us, length us, event | category | flops | bytes accessed | tf_op | source)
XLA Modules:
  0.0 61.1 jit_solution(5249395390764954847)
XLA Ops:
  0.0 59.0 %shard_map.64 = bf16[96,4096]{1,0:T(8,128)(2,1)} custom-call(s32[128]{0:T(128)} %span_hbm.1, s32[1,128]{1,0:T(1,128)} %bitcast.3, s32[96,128]{1,0:T(8,128)} %bitcast.2, bf16[192,2048]{1,0:T(8,128)(2,1)} %q_hbm.1, bf16[192,512]{1,0:T(8,128)(2,1)} %k_hbm.1, bf16[192,512]{1,0:T(8,128)(2,1)} %v_hbm.1, bf16[2048,4096]{1,0:T(8,128)(2,1)} %w_hbm.1), custom_call_target="tpu_custom_call" | custom-call | tf_op jit(solution)/shard_map/pallas_call | solution.py:433
  59.1 2.1 %copy.8 = bf16[96,4096]{1,0:T(8,128)(2,1)} copy(bf16[96,4096]{1,0:T(8,128)(2,1)} %shard_map.64) | data formatting | bytes 1572864

commit v6 on v5

--- a/solution.py
+++ b/solution.py
@@ -218,13 +218,15 @@
         for i in EARLY:
             from_across(i)
         for i in LATE:
+            last(i, 0, x)
+        for i in LATE:
             from_far(i, 0, z)
         for i in EARLY:
             from_side(i, 0, z)
         for k, i in enumerate(EARLY):
             from_side(i, 1, zp)
             extra(k)
-        for n, xo in enumerate((x, x_left, x_right)):
+        for n, xo in ((1, x_left), (2, x_right)):
             for i in LATE:
                 last(i, n, xo)
         for k, i in enumerate(EARLY):

time: 61.3 us -> 61.3 us (level)
  no operation moved by 1% of the time
where the time goes in v6:
time: 61.3 us; the launch traced here: 61.1 us
  Pallas kernels  59 us (96%)
  local copies, waits for them, and re-layouts  2.06 us (3%)
    pallas_call x1, Pallas kernels, local(): pl.pallas_call(kernel, out_shape=jax.ShapeDtypeStruct((SPAN, model), bf16...  59 us
    unnamed x1, local copies, waits for them, and re-layouts  2.06 us

profile of v6, /device:TPU:17, one launch (start us, length us, event | category | flops | bytes accessed | tf_op | source)
XLA Modules:
  0.0 61.1 jit_solution(3156208066135950029)
XLA Ops:
  0.0 59.0 %shard_map.64 = bf16[96,4096]{1,0:T(8,128)(2,1)} custom-call(s32[128]{0:T(128)} %span_hbm.1, s32[1,128]{1,0:T(1,128)} %bitcast.3, s32[96,128]{1,0:T(8,128)} %bitcast.2, bf16[192,2048]{1,0:T(8,128)(2,1)} %q_hbm.1, bf16[192,512]{1,0:T(8,128)(2,1)} %k_hbm.1, bf16[192,512]{1,0:T(8,128)(2,1)} %v_hbm.1, bf16[2048,4096]{1,0:T(8,128)(2,1)} %w_hbm.1), custom_call_target="tpu_custom_call" | custom-call | tf_op jit(solution)/shard_map/pallas_call | solution.py:435
  59.0 2.1 %copy.8 = bf16[96,4096]{1,0:T(8,128)(2,1)} copy(bf16[96,4096]{1,0:T(8,128)(2,1)} %shard_map.64) | data formatting | bytes 1572864
